TPU v7x, 32 devices: a whole 2x2x4 slice. The times are simulated.
32 devices in a mesh: scene: 2 (over y), pulse: 4 (over z), rng: 2 (over core), pol: 2 (over x).
Axes of the slice: x: 2, y: 2, z: 4, core: 2. Of those that a mesh axis runs over, the one named last changes fastest.
Arguments:
- echoes: bfloat16 [8, 2, 128, 8192], P(('scene', 'pol'), None, None, ('pulse', 'rng')), parts along dimension 0, may hold values from -6 to 6
- migration: int32 [32, 8192], P(('scene', 'pulse', 'rng')), parts along dimension 0, may hold values from 0 to 8
- fm_rate: float32 [256], P(('scene', 'pulse', 'rng')), parts along dimension 0, may hold values from 0.05 to 0.2
Outputs:
- coherency: bfloat16 [9, 256, 8192], P(None, ('scene', 'pulse', 'rng'), 'pol'), parts along dimension 1
There are 2 independent parts, one for each index of `scene`. A program takes and returns all parts, laid end to end along the dimension named above; each array names one. Nothing has to cross between parts.
Inputs may be any that keep to these rules, and one draw needn't show every extreme that they name: migration[b, f] is the shift in bins for range bins b * 8 to (b + 1) * 8 - 1 at azimuth frequency bin f.
All inputs are finite; a program needn't handle non-finite values.
Results may differ from a plain program's by a relative error of at most 0.006.
Values may be sent and summed in bfloat16 or wider, within the bound.
A program may use at most 64 MiB of HBM per device.

v0:
```python
import functools
import math

import jax
import jax.numpy as jnp
import numpy as np
from jax import lax
from jax.experimental import pallas as pl
from jax.experimental.pallas import tpu as pltpu
from jax.sharding import PartitionSpec as P

RBLK = 8
SMAX = 8
WIN = 7
HALF = WIN // 2
LANES = 128
STEP = 4
SLOTS = 3
ROOT_HALF = 0.7071067811865476
MESH = pl.DeviceIdType.MESH
F32 = jnp.float32
BF16 = jnp.bfloat16


def fit(function, degree):
    nodes = (np.cos(np.pi * (np.arange(64) + 0.5) / 64) + 1) / 8
    poly = np.polynomial.Chebyshev.fit(nodes, function(nodes), degree, domain=[0, 0.25])
    return [float(v) for v in poly.convert(kind=np.polynomial.Polynomial).coef]


SIN_COEF = fit(lambda y: np.sin(2 * np.pi * np.sqrt(y)) / np.sqrt(y), 7)
COS_COEF = fit(lambda y: np.cos(2 * np.pi * np.sqrt(y)), 7)


def horner(coefs, y):
    total = jnp.full_like(y, coefs[-1])
    for coef in coefs[-2::-1]:
        total = total * y + coef
    return total


def trig(period, height, width):
    index = np.arange(height)[:, None] * np.arange(width)[None, :] % period
    return np.cos(2 * np.pi * index / period), np.sin(2 * np.pi * index / period)


def tables(outer):
    size = outer * LANES
    oc, os_ = trig(outer, outer, outer)
    scale = 1.0 / math.sqrt(outer)
    first = np.block([[oc, os_], [-os_, oc]]) * scale
    last = np.block([[oc, -os_], [os_, oc]]) * scale
    ic, is_ = trig(LANES, LANES, LANES)
    fwd = np.block([[ic, -is_], [is_, ic]])
    inv = np.block([[ic, is_], [-is_, ic]])
    tc, ts = trig(size, outer, LANES)
    row = np.arange(LANES)
    gap = row[:, None] - row[None, :]
    near = np.abs(gap) <= HALF
    wrap = np.abs(np.abs(gap) - LANES) <= HALF
    band = np.concatenate([near, wrap], axis=0)
    per_row = LANES // outer
    spread = np.zeros((per_row * outer, LANES))
    for u in range(outer):
        for h in range(per_row):
            spread[h * outer + u, per_row * u + h] = 1
    short = lambda v: np.asarray(v, np.float32).astype(BF16).astype(np.float32)

    def gain(v):
        return float(np.sum(v * short(v)) / np.sum(v * v))

    root = math.sqrt(LANES)
    there, back = root * gain(first) * gain(fwd), root * gain(inv) * gain(last)
    twiddle = np.stack([tc / there, ts / there, tc / back, ts / back])
    fill = lambda v, width: np.pad(v, ((0, 0), (0, width - v.shape[1])))
    slim = np.concatenate([fill(first, LANES), fill(last, LANES), spread])
    wide = np.concatenate([fwd, inv, fill(band, 2 * LANES)])
    return jnp.asarray(wide, BF16), jnp.asarray(slim, BF16), jnp.asarray(twiddle, F32)


def kernel(
    chans, groups, pols, bins, outer, rng_size,
    echo, mig_hbm, rate, wide_hbm, slim_hbm, twiddle_hbm,
    out,
    mig, wide_t, slim_t, twiddle, t_sem,
    recv, unpacked, spec, image, edge, quad, quad_edge, shifts, mig_rows, cosine, sine,
    cells, cells_edge, padded, result,
    z_send, z_recv, h_send, h_recv, x_send, x_recv, e_send, e_recv, r_send, r_recv, f_send, f_recv,
):
    half_rows = outer // pols
    local_a = outer // groups
    pulse_i, rng_i, pol_i = (lax.axis_index(n) for n in ("pulse", "rng", "pol"))
    me = pulse_i * rng_size + rng_i

    def member(q):
        return {"pulse": q // rng_size, "rng": lax.rem(q, rng_size)}

    fetches = [
        pltpu.make_async_copy(source, target, t_sem.at[i])
        for i, (source, target) in enumerate(
            ((mig_hbm, mig), (slim_hbm, slim_t), (twiddle_hbm, twiddle), (wide_hbm, wide_t))
        )
    ]
    for fetch in fetches:
        fetch.start()
    two = 2 * outer
    first_t, last_t = slim_t.at[0:two, 0:two], slim_t.at[two : 2 * two, 0:two]
    fwd_t, inv_t = wide_t.at[0 : 2 * LANES], wide_t.at[2 * LANES : 4 * LANES]
    band = wide_t.at[4 * LANES : 6 * LANES, 0:LANES]

    barrier = pltpu.get_barrier_semaphore()

    def greet_group(k, carry):
        pl.semaphore_signal(
            barrier, inc=1, device_id=member(lax.rem(me + k, groups)), device_id_type=MESH
        )
        return carry

    lax.fori_loop(1, groups, greet_group, 0)
    for k in range(1, pols):
        pl.semaphore_signal(
            barrier, inc=1, device_id={"pol": lax.rem(pol_i + k, pols)}, device_id_type=MESH
        )
    pl.semaphore_wait(barrier, groups - 1 + pols - 1)

    depth = groups // rng_size

    def z_copy(ch, q, slot):
        return pltpu.make_async_remote_copy(
            src_ref=echo.at[ch, :, pl.ds(pl.multiple_of(q * bins, bins), bins), :],
            dst_ref=recv.at[ch, slot],
            send_sem=z_send.at[ch, q],
            recv_sem=z_recv.at[ch, slot],
            device_id=member(q),
            device_id_type=MESH,
        )

    def own_copy(ch):
        return pltpu.make_async_copy(
            echo.at[ch, :, pl.ds(pl.multiple_of(me * bins, bins), bins), :],
            recv.at[ch, me],
            z_recv.at[ch, me],
        )

    for ch in range(chans):

        def send_echo(i, carry, ch=ch):
            gap = depth - 1 - i
            for sign in (1, -1):
                layer = pulse_i + sign * gap

                @pl.when((layer >= 0) & (layer < depth))
                def _(layer=layer):
                    for j in range(rng_size):
                        q = layer * rng_size + lax.rem(rng_i + j, rng_size)
                        z_copy(ch, q, me).start()

            return carry

        lax.fori_loop(0, depth - 1, send_echo, 0)
        for j in range(1, rng_size):
            q = pulse_i * rng_size + lax.rem(rng_i + j, rng_size)
            z_copy(ch, q, me).start()
        own_copy(ch).start()

    def zero_edges():
        @pl.when(me == groups - 1)
        def _():
            spec[:, :, bins:, :, :] = jnp.zeros((chans, 2, SMAX, outer, LANES), BF16)
            quad[:, :, HALF + bins :, :, :] = jnp.zeros((4, 2, HALF, half_rows, LANES), BF16)
            quad_edge[:, :, HALF + bins :, :, :] = jnp.zeros((4, 2, HALF, 2, LANES), F32)

        @pl.when(me == 0)
        def _():
            quad[:, :, :HALF, :, :] = jnp.zeros((4, 2, HALF, half_rows, LANES), BF16)
            quad_edge[:, :, :HALF, :, :] = jnp.zeros((4, 2, HALF, 2, LANES), F32)

    zero_edges()
    for fetch in fetches:
        fetch.wait()

    per_row = LANES // outer
    for k in range(mig.shape[0]):
        for u in range(outer):
            mig_rows[u : u + 1, :] = mig[k : k + 1, u * LANES : (u + 1) * LANES].astype(F32)
        turned = mig_rows[...].T.astype(BF16)
        total = jnp.zeros((outer, LANES), F32)
        for h in range(per_row):
            total = total + jnp.dot(
                turned[h * outer : (h + 1) * outer],
                slim_t[(2 * two + h * outer) : (2 * two + (h + 1) * outer)],
                preferred_element_type=F32,
            )
        shifts[k] = total.astype(BF16)

    size = outer * LANES
    position = lax.broadcasted_iota(jnp.int32, (outer, LANES), 0) + outer * (
        lax.broadcasted_iota(jnp.int32, (outer, LANES), 1)
    )
    centred = jnp.where(position < size // 2, position, position - size).astype(F32)
    quadratic = centred * centred / size

    def phase_row(r, carry):
        turns = (0.5 * rate[r]) * quadratic
        turns = turns - jnp.round(turns)
        square = turns * turns
        cosine[r] = horner(COS_COEF, square)
        sine[r] = horner(SIN_COEF, square) * turns
        return carry

    lax.fori_loop(0, bins, phase_row, 0)

    def halo_copy(ch, part):
        return pltpu.make_async_remote_copy(
            src_ref=spec.at[ch, :, pl.ds(part * STEP, STEP)],
            dst_ref=spec.at[ch, :, pl.ds(bins + part * STEP, STEP)],
            send_sem=h_send.at[ch, part],
            recv_sem=h_recv.at[ch, part],
            device_id=member(jnp.maximum(me - 1, 0)),
            device_id_type=MESH,
        )

    def x_copy(ch, blk, dest, owner):
        rows = pl.ds(HALF + blk * STEP, STEP)
        return pltpu.make_async_remote_copy(
            src_ref=image.at[ch, dest, :, pl.ds(blk * STEP, STEP)],
            dst_ref=quad.at[owner * chans + ch, :, rows],
            send_sem=x_send.at[ch, blk, dest],
            recv_sem=x_recv.at[ch, blk, owner],
            device_id={"pol": dest},
            device_id_type=MESH,
        )

    def e_copy(ch, dest, owner):
        return pltpu.make_async_remote_copy(
            src_ref=edge.at[ch, dest],
            dst_ref=quad_edge.at[owner * chans + ch, :, pl.ds(HALF, bins)],
            send_sem=e_send.at[ch, dest],
            recv_sem=e_recv.at[ch, owner],
            device_id={"pol": dest},
            device_id_type=MESH,
        )

    def x_own(ch, blk):
        return pltpu.make_async_copy(
            image.at[ch, pol_i, :, pl.ds(blk * STEP, STEP)],
            quad.at[pol_i * chans + ch, :, pl.ds(HALF + blk * STEP, STEP)],
            x_recv.at[ch, blk, pol_i],
        )

    def e_own(ch):
        return pltpu.make_async_copy(
            edge.at[ch, pol_i],
            quad_edge.at[pol_i * chans + ch, :, pl.ds(HALF, bins)],
            e_recv.at[ch, pol_i],
        )

    def relay(array, sems, recvs, chan, side):
        take = HALF if side == 0 else bins
        put = HALF + bins if side == 0 else 0
        target = jnp.maximum(me - 1, 0) if side == 0 else jnp.minimum(me + 1, groups - 1)
        return pltpu.make_async_remote_copy(
            src_ref=array.at[chan, :, pl.ds(take, HALF)],
            dst_ref=array.at[chan, :, pl.ds(put, HALF)],
            send_sem=sems.at[chan, side],
            recv_sem=recvs.at[chan, side],
            device_id=member(target),
            device_id_type=MESH,
        )

    def unpack(ch):
        def body(p, carry):
            z_copy(ch, p, p).wait_recv()
            for part in range(2):
                for a in range(local_a):
                    tile = recv[ch, p, part, :, a * LANES : (a + 1) * LANES].astype(F32)
                    start = pl.multiple_of((part * outer + p * local_a + a) * bins, bins)
                    unpacked[pl.ds(start, bins), :] = tile
            return carry

        lax.fori_loop(0, groups, body, 0)

    def forward(ch, g):
        rows = [unpacked[pl.ds(g * STEP + j, 2 * outer, stride=bins), :] for j in range(STEP)]
        wide = jnp.concatenate([row.astype(BF16) for row in rows], axis=1)
        mid = jnp.dot(first_t[...], wide, preferred_element_type=F32)
        tc, ts = twiddle[0], twiddle[1]
        turned = []
        for j in range(STEP):
            re = mid[:outer, j * LANES : (j + 1) * LANES]
            im = mid[outer:, j * LANES : (j + 1) * LANES]
            turned.append(
                jnp.concatenate(
                    [(re * tc + im * ts).astype(BF16), (im * tc - re * ts).astype(BF16)], axis=1
                )
            )
        done = jnp.dot(
            jnp.concatenate(turned, axis=0), fwd_t[...], preferred_element_type=F32
        ).astype(BF16)
        for j in range(STEP):
            r = g * STEP + j
            spec[ch, 0, r] = done[j * outer : (j + 1) * outer, :LANES]
            spec[ch, 1, r] = done[j * outer : (j + 1) * outer, LANES:]

    def inverse(ch, blk, g):
        amount = shifts[blk]
        turned = []
        for j in range(STEP):
            r = g * STEP + j
            re, im = spec[ch, 0, r], spec[ch, 1, r]
            for s in range(1, SMAX + 1):
                hit = amount == s
                re = jnp.where(hit, spec[ch, 0, r + s], re)
                im = jnp.where(hit, spec[ch, 1, r + s], im)
            re, im = re.astype(F32), im.astype(F32)
            c, s_ = cosine[r], sine[r]
            turned.append(
                jnp.concatenate(
                    [(re * c - im * s_).astype(BF16), (re * s_ + im * c).astype(BF16)], axis=1
                )
            )
        mid = jnp.dot(jnp.concatenate(turned, axis=0), inv_t[...], preferred_element_type=F32)
        tc, ts = twiddle[2], twiddle[3]
        columns = []
        for j in range(STEP):
            re = mid[j * outer : (j + 1) * outer, :LANES]
            im = mid[j * outer : (j + 1) * outer, LANES:]
            columns.append(
                jnp.concatenate(
                    [(re * tc - im * ts).astype(BF16), (im * tc + re * ts).astype(BF16)], axis=0
                )
            )
        done = jnp.dot(
            last_t[...], jnp.concatenate(columns, axis=1), preferred_element_type=F32
        )
        for j in range(STEP):
            for part in range(2):
                full = done[part * outer : (part + 1) * outer, j * LANES : (j + 1) * LANES]
                r = g * STEP + j
                zero = jnp.zeros((1, LANES), F32)
                rounded = full.astype(BF16)
                exact = rounded.astype(F32)
                for h in range(pols):
                    low, high = h * half_rows, (h + 1) * half_rows
                    image[ch, h, part, r] = rounded[low:high]
                    before = exact[low - 1 : low] if h > 0 else zero
                    after = exact[high : high + 1] if h < pols - 1 else zero
                    edge[ch, h, part, r, 0:1] = before
                    edge[ch, h, part, r, 1:2] = after

    def loop(count, start, fun):
        def body(i, carry):
            fun(start + i)
            return carry

        lax.fori_loop(0, count, body, 0)

    sides = ((0, me > 0), (1, me < groups - 1))

    def relays(array, sems, recvs, ch, side):
        @pl.when(sides[side][1])
        def _():
            for o in range(pols):
                relay(array, sems, recvs, o * chans + ch, side).start()

    quads = bins // STEP

    def finish_exchange(ch):
        for quad_i in range(quads):
            for o in range(pols):
                x_copy(ch, quad_i, o, o).wait_recv()
            if quad_i == 0:
                relays(quad, r_send, r_recv, ch, 0)
        relays(quad, r_send, r_recv, ch, 1)
        for o in range(pols):
            e_copy(ch, o, o).wait_recv()
        for side in range(2):
            relays(quad_edge, f_send, f_recv, ch, side)

    for ch in range(chans):
        unpack(ch)
        for part in range(SMAX // STEP):
            forward(ch, part)

            @pl.when(me > 0)
            def _(ch=ch, part=part):
                halo_copy(ch, part).start()

        for g in range(SMAX // STEP, quads):
            forward(ch, g)
        if ch > 0:
            finish_exchange(ch - 1)
        for quad_i in range(quads):
            late = quad_i - (quads - SMAX // STEP)
            if late >= 0:

                @pl.when(me < groups - 1)
                def _(ch=ch, late=late):
                    halo_copy(ch, late).wait_recv()

            inverse(ch, quad_i * STEP // RBLK, quad_i)
            if quad_i == quads - 1:
                for k in range(1, pols):
                    e_copy(ch, lax.rem(pol_i + k, pols), pol_i).start()
                e_own(ch).start()
            for k in range(1, pols):
                x_copy(ch, quad_i, lax.rem(pol_i + k, pols), pol_i).start()
            x_own(ch, quad_i).start()

    finish_exchange(chans - 1)

    def pauli(source, target, r):
        v = [[source[c, part, r].astype(F32) for part in range(2)] for c in range(4)]
        k1 = [(v[0][i] + v[3][i]) * ROOT_HALF for i in range(2)]
        k2 = [(v[0][i] - v[3][i]) * ROOT_HALF for i in range(2)]
        k3 = [(v[1][i] + v[2][i]) * ROOT_HALF for i in range(2)]
        terms = [k[0] * k[0] + k[1] * k[1] for k in (k1, k2, k3)]
        for a, b in ((k1, k2), (k1, k3), (k2, k3)):
            terms.append(a[0] * b[0] + a[1] * b[1])
            terms.append(a[1] * b[0] - a[0] * b[1])
        for i, term in enumerate(terms):
            target[i, r] = term

    def cell_row(r):
        pauli(quad, cells, r)
        pauli(quad_edge, cells_edge, r)

    loop(bins, HALF, cell_row)
    for side, cond in ((0, me < groups - 1), (1, me > 0)):

        @pl.when(cond)
        def _(side=side):
            for chan in range(4):
                relay(quad, r_send, r_recv, chan, side).wait_recv()
                relay(quad_edge, f_send, f_recv, chan, side).wait_recv()

    loop(HALF, 0, cell_row)
    loop(HALF, bins + HALF, cell_row)

    def range_sum(x):
        two = x[:-1] + x[1:]
        four = two[:-2] + two[2:]
        return four[:bins] + two[4 : 4 + bins] + x[6 : 6 + bins]

    lane = lax.broadcasted_iota(jnp.int32, (bins, half_rows, LANES), 2)

    def component(i):
        slot = i % SLOTS
        for j in range(half_rows // 8):
            padded[slot, :, 8 + j * 8 : 16 + j * 8, :] = range_sum(cells[i, :, j * 8 : (j + 1) * 8, :])
        rim = range_sum(cells_edge[i])
        padded[slot, :, 7:8, :] = rim[:, 0:1, :]
        padded[slot, :, 8 + half_rows : 9 + half_rows, :] = rim[:, 1:2, :]
        mid = padded[slot, :, 8 : 8 + half_rows, :]
        side = jnp.where(
            lane < LANES // 2,
            padded[slot, :, 9 : 9 + half_rows, :],
            padded[slot, :, 7 : 7 + half_rows, :],
        )
        flat = (bins * half_rows, LANES)
        both = jnp.concatenate(
            [mid.reshape(flat).astype(BF16), side.reshape(flat).astype(BF16)], axis=1
        )
        total = jnp.dot(both, band[...], preferred_element_type=F32)
        result[slot] = total * (1.0 / (WIN * WIN))
        for a in range(half_rows):
            piece = result[slot, pl.ds(a, bins, stride=half_rows), :]
            out[i, :, a * LANES : (a + 1) * LANES] = piece.astype(BF16)

    for i in range(9):
        component(i)

    for ch in range(chans):

        def sent(k, carry, ch=ch):
            z_copy(ch, lax.rem(me + k, groups), me).wait_send()
            return carry

        lax.fori_loop(1, groups, sent, 0)

        @pl.when(me > 0)
        def _(ch=ch):
            for part in range(SMAX // STEP):
                halo_copy(ch, part).wait_send()

        for k in range(1, pols):
            dest = lax.rem(pol_i + k, pols)
            for quad_i in range(quads):
                x_copy(ch, quad_i, dest, pol_i).wait_send()
            e_copy(ch, dest, pol_i).wait_send()

    for side, cond in sides:

        @pl.when(cond)
        def _(side=side):
            for chan in range(4):
                relay(quad, r_send, r_recv, chan, side).wait_send()
                relay(quad_edge, f_send, f_recv, chan, side).wait_send()


def shards(echoes, migration, fm_rate):
    rng_size = lax.axis_size("rng")
    groups = lax.axis_size("pulse") * rng_size
    pols = lax.axis_size("pol")
    chans = echoes.shape[0]
    pulses = echoes.shape[3]
    bins = echoes.shape[2] // groups
    outer = groups * pulses // LANES
    half_rows = outer // pols
    consts = tables(outer)
    vmem = pl.BlockSpec(memory_space=pltpu.VMEM)
    anywhere = pl.BlockSpec(memory_space=pltpu.HBM)
    dma = pltpu.SemaphoreType.DMA
    tall = bins + 2 * HALF
    return pl.pallas_call(
        functools.partial(kernel, chans, groups, pols, bins, outer, rng_size),
        out_shape=pltpu.VMEM((9, bins, half_rows * LANES), BF16),
        in_specs=[
            anywhere,
            anywhere,
            pl.BlockSpec(memory_space=pltpu.SMEM),
        ]
        + [anywhere] * len(consts),
        out_specs=vmem,
        scratch_shapes=[
            pltpu.VMEM(migration.shape, jnp.int32),
            *(pltpu.VMEM(table.shape, table.dtype) for table in consts),
            dma((1 + len(consts),)),
            pltpu.VMEM((chans, groups, 2, bins, pulses), BF16),
            pltpu.VMEM((2 * outer * bins, LANES), F32),
            pltpu.VMEM((chans, 2, bins + SMAX, outer, LANES), BF16),
            pltpu.VMEM((chans, pols, 2, bins, half_rows, LANES), BF16),
            pltpu.VMEM((chans, pols, 2, bins, 2, LANES), F32),
            pltpu.VMEM((4, 2, tall, half_rows, LANES), BF16),
            pltpu.VMEM((4, 2, tall, 2, LANES), F32),
            pltpu.VMEM((migration.shape[0], outer, LANES), BF16),
            pltpu.VMEM((outer, LANES), F32),
            pltpu.VMEM((bins, outer, LANES), F32),
            pltpu.VMEM((bins, outer, LANES), F32),
            pltpu.VMEM((9, tall, half_rows, LANES), F32),
            pltpu.VMEM((9, tall, 2, LANES), F32),
            pltpu.VMEM((SLOTS, bins, half_rows + 16, LANES), F32),
            pltpu.VMEM((SLOTS, bins * half_rows, LANES), F32),
            dma((chans, groups)),
            dma((chans, groups)),
            dma((chans, SMAX // STEP)),
            dma((chans, SMAX // STEP)),
            dma((chans, bins // STEP, pols)),
            dma((chans, bins // STEP, pols)),
            dma((chans, pols)),
            dma((chans, pols)),
            dma((4, 2)),
            dma((4, 2)),
            dma((4, 2)),
            dma((4, 2)),
        ],
        compiler_params=pltpu.CompilerParams(
            collective_id=0, has_side_effects=True, vmem_limit_bytes=58 * 1024 * 1024
        ),
    )(echoes, migration, fm_rate, *consts)


def solution(mesh):
    placed = (
        P(("scene", "pol"), None, None, ("pulse", "rng")),
        P(("scene", "pulse", "rng"), None),
        P(("scene", "pulse", "rng")),
    )
    return jax.shard_map(
        shards,
        mesh=mesh,
        in_specs=placed,
        out_specs=P(None, ("scene", "pulse", "rng"), "pol"),
        check_vma=False,
    )
```

profile of v0, /device:TPU:13, one launch (start us, length us, event | category | flops | bytes accessed | tf_op | source)
XLA Modules:
  0.0 48.8 jit_solution(16954415783535396645)
XLA Ops:
  0.0 47.8 %shard_map.64 = bf16[9,16,4096]{2,1,0:T(8,128)(2,1)S(1)} custom-call(bf16[2,2,128,1024]{3,2,1,0:T(8,128)(2,1)} %echo.1, s32[2,8192]{1,0:T(2,128)} %mig_hbm.1, f32[16]{0:T(128)} %rate.1, bf16[768,256]{1,0:T(8,128)(2,1)} %constant.6.clone.wide_hbm, bf16[384,128]{1,0:T(8,128)(2,1)} %constant.7.clone.slim_hbm, f32[4,64,128]{2,1,0:T(8,128)} %constant.8.clone.twiddle_hbm), custom_call_target="tpu_custom_call" | custom-call | tf_op jit(solution)/shard_map/pallas_call | solution.py:515
  47.8 1.0 %copy.8 = bf16[9,16,4096]{2,1,0:T(8,128)(2,1)} copy(bf16[9,16,4096]{2,1,0:T(8,128)(2,1)S(1)} %shard_map.64) | data formatting | bytes 2359296
where the time goes:
time: 48.9 us; the launch traced here: 48.8 us
  Pallas kernels  47.8 us (98%)
  local copies, waits for them, and re-layouts  1.02 us (2%)
    pallas_call x1, Pallas kernels, shards(): pl.pallas_call(functools.partial(kernel, chans, groups, pols, bins, outer...  47.8 us
    unnamed x1, local copies, waits for them, and re-layouts  1.02 us

commit v1 on v0

--- a/solution.py
+++ b/solution.py
@@ -16,6 +16,11 @@
 LANES = 128
 STEP = 4
 SLOTS = 3
+AHEAD = 3
+LAG = 1
+FIRST = 0
+RAW = 1
+DRAIN = AHEAD + LAG + FIRST
 ROOT_HALF = 0.7071067811865476
 MESH = pl.DeviceIdType.MESH
 F32 = jnp.float32
@@ -124,44 +129,88 @@
     pl.semaphore_wait(barrier, groups - 1 + pols - 1)
 
     depth = groups // rng_size
-
-    def z_copy(ch, q, slot):
+    quads = bins // STEP
+    halos = SMAX // STEP
+    units = chans * quads
+    mid = rng_size * (depth // 2)
+
+    def z_copy(unit, first, slot, q):
+        ch, part = unit // quads, lax.rem(unit, quads)
+        start = pl.multiple_of(first * bins + part * STEP, STEP)
         return pltpu.make_async_remote_copy(
-            src_ref=echo.at[ch, :, pl.ds(pl.multiple_of(q * bins, bins), bins), :],
-            dst_ref=recv.at[ch, slot],
-            send_sem=z_send.at[ch, q],
-            recv_sem=z_recv.at[ch, slot],
+            src_ref=echo.at[ch, :, pl.ds(start, STEP), :],
+            dst_ref=recv.at[slot, me],
+            send_sem=z_send.at[slot],
+            recv_sem=z_recv.at[slot],
             device_id=member(q),
             device_id_type=MESH,
         )
 
-    def own_copy(ch):
+    def own_copy(unit, first, slot):
+        ch, part = unit // quads, lax.rem(unit, quads)
+        start = pl.multiple_of(first * bins + part * STEP, STEP)
         return pltpu.make_async_copy(
-            echo.at[ch, :, pl.ds(pl.multiple_of(me * bins, bins), bins), :],
-            recv.at[ch, me],
-            z_recv.at[ch, me],
-        )
-
-    for ch in range(chans):
-
-        def send_echo(i, carry, ch=ch):
+            echo.at[ch, :, pl.ds(start, STEP), :], recv.at[slot, me], z_recv.at[slot]
+        )
+
+    def z_landed(slot):
+        pltpu.make_async_copy(recv.at[slot], recv.at[slot], z_recv.at[slot]).wait()
+
+    def z_sent(slot):
+        some = recv.at[slot, pl.ds(0, groups - 1)]
+        pltpu.make_async_copy(some, some, z_send.at[slot]).wait()
+
+    def send_step(step):
+        def to_layer(layer, near):
+            for j in range(rng_size):
+                q = layer * rng_size + j
+                unit = step - LAG * j - FIRST * jnp.minimum(layer, 1)
+                valid = (unit >= 0) & (unit < units)
+                if near:
+
+                    @pl.when(valid & (rng_i == j))
+                    def _():
+                        own_copy(unit, me, unit).start()
+
+                    valid = valid & (rng_i != j)
+
+                @pl.when(valid)
+                def _():
+                    z_copy(unit, q, unit, q).start()
+
+        def send_echo(i, carry):
             gap = depth - 1 - i
             for sign in (1, -1):
                 layer = pulse_i + sign * gap
 
                 @pl.when((layer >= 0) & (layer < depth))
                 def _(layer=layer):
-                    for j in range(rng_size):
-                        q = layer * rng_size + lax.rem(rng_i + j, rng_size)
-                        z_copy(ch, q, me).start()
+                    to_layer(layer, False)
 
             return carry
 
         lax.fori_loop(0, depth - 1, send_echo, 0)
-        for j in range(1, rng_size):
-            q = pulse_i * rng_size + lax.rem(rng_i + j, rng_size)
-            z_copy(ch, q, me).start()
-        own_copy(ch).start()
+        to_layer(pulse_i, True)
+        early = step - LAG - FIRST - RAW
+        slot = units + early // quads * halos + lax.rem(early, quads)
+        valid = (early >= 0) & (early < units) & (lax.rem(early, quads) < halos)
+        if mid > 0:
+
+            @pl.when(valid & (me == mid - 1))
+            def _():
+                own_copy(early, mid, slot).start()
+
+            @pl.when(valid & (me != mid - 1))
+            def _():
+                z_copy(early, mid, slot, mid - 1).start()
+
+    mylag = LAG * rng_i + FIRST * jnp.minimum(pulse_i, 1)
+
+    def opening(step, carry):
+        send_step(step)
+        return carry
+
+    lax.fori_loop(0, AHEAD + mylag, opening, 0)
 
     def zero_edges():
         @pl.when(me == groups - 1)
@@ -220,40 +269,39 @@
             device_id_type=MESH,
         )
 
-    def x_copy(ch, blk, dest, owner):
-        rows = pl.ds(HALF + blk * STEP, STEP)
+    def x_copy(ch, blk, k):
         return pltpu.make_async_remote_copy(
-            src_ref=image.at[ch, dest, :, pl.ds(blk * STEP, STEP)],
-            dst_ref=quad.at[owner * chans + ch, :, rows],
-            send_sem=x_send.at[ch, blk, dest],
-            recv_sem=x_recv.at[ch, blk, owner],
-            device_id={"pol": dest},
+            src_ref=image.at[ch, k - 1, :, pl.ds(blk * STEP, STEP)],
+            dst_ref=quad.at[pol_i * chans + ch, :, pl.ds(HALF + blk * STEP, STEP)],
+            send_sem=x_send.at[ch],
+            recv_sem=x_recv.at[ch, blk],
+            device_id={"pol": lax.rem(pol_i + k, pols)},
             device_id_type=MESH,
         )
 
-    def e_copy(ch, dest, owner):
+    def e_copy(ch, blk, k):
         return pltpu.make_async_remote_copy(
-            src_ref=edge.at[ch, dest],
-            dst_ref=quad_edge.at[owner * chans + ch, :, pl.ds(HALF, bins)],
-            send_sem=e_send.at[ch, dest],
-            recv_sem=e_recv.at[ch, owner],
-            device_id={"pol": dest},
+            src_ref=edge.at[ch, k - 1, :, pl.ds(blk * STEP, STEP)],
+            dst_ref=quad_edge.at[pol_i * chans + ch, :, pl.ds(HALF + blk * STEP, STEP)],
+            send_sem=e_send.at[ch],
+            recv_sem=e_recv.at[ch, blk],
+            device_id={"pol": lax.rem(pol_i + k, pols)},
             device_id_type=MESH,
         )
 
-    def x_own(ch, blk):
-        return pltpu.make_async_copy(
-            image.at[ch, pol_i, :, pl.ds(blk * STEP, STEP)],
-            quad.at[pol_i * chans + ch, :, pl.ds(HALF + blk * STEP, STEP)],
-            x_recv.at[ch, blk, pol_i],
-        )
-
-    def e_own(ch):
-        return pltpu.make_async_copy(
-            edge.at[ch, pol_i],
-            quad_edge.at[pol_i * chans + ch, :, pl.ds(HALF, bins)],
-            e_recv.at[ch, pol_i],
-        )
+    def landed(ch, blk):
+        if pols > 1:
+            rows = pl.ds(HALF + blk * STEP, STEP)
+            some = quad.at[pl.ds(0, pols - 1), :, rows]
+            few = quad_edge.at[pl.ds(0, pols - 1), :, rows]
+            pltpu.make_async_copy(some, some, x_recv.at[ch, blk]).wait()
+            pltpu.make_async_copy(few, few, e_recv.at[ch, blk]).wait()
+
+    def x_sent(ch):
+        if pols > 1:
+            some, few = image.at[ch], edge.at[ch]
+            pltpu.make_async_copy(some, some, x_send.at[ch]).wait()
+            pltpu.make_async_copy(few, few, e_send.at[ch]).wait()
 
     def relay(array, sems, recvs, chan, side):
         take = HALF if side == 0 else bins
@@ -262,33 +310,42 @@
         return pltpu.make_async_remote_copy(
             src_ref=array.at[chan, :, pl.ds(take, HALF)],
             dst_ref=array.at[chan, :, pl.ds(put, HALF)],
-            send_sem=sems.at[chan, side],
-            recv_sem=recvs.at[chan, side],
+            send_sem=sems.at[side],
+            recv_sem=recvs.at[side],
             device_id=member(target),
             device_id_type=MESH,
         )
 
-    def unpack(ch):
+    sides = ((0, me > 0), (1, me < groups - 1))
+
+    def relayed(array, sems):
+        rows = array.at[:, :, pl.ds(0, HALF)]
+        for side, cond in sides:
+
+            @pl.when(cond)
+            def _(side=side):
+                pltpu.make_async_copy(rows, rows, sems.at[side]).wait()
+
+    def unpack(slot):
         def body(p, carry):
-            z_copy(ch, p, p).wait_recv()
             for part in range(2):
                 for a in range(local_a):
-                    tile = recv[ch, p, part, :, a * LANES : (a + 1) * LANES].astype(F32)
-                    start = pl.multiple_of((part * outer + p * local_a + a) * bins, bins)
-                    unpacked[pl.ds(start, bins), :] = tile
+                    tile = recv[slot, p, part, :, a * LANES : (a + 1) * LANES].astype(F32)
+                    start = pl.multiple_of((part * outer + p * local_a + a) * STEP, STEP)
+                    unpacked[pl.ds(start, STEP), :] = tile
             return carry
 
         lax.fori_loop(0, groups, body, 0)
 
     def forward(ch, g):
-        rows = [unpacked[pl.ds(g * STEP + j, 2 * outer, stride=bins), :] for j in range(STEP)]
+        rows = [unpacked[pl.ds(j, 2 * outer, stride=STEP), :] for j in range(STEP)]
         wide = jnp.concatenate([row.astype(BF16) for row in rows], axis=1)
-        mid = jnp.dot(first_t[...], wide, preferred_element_type=F32)
+        half = jnp.dot(first_t[...], wide, preferred_element_type=F32)
         tc, ts = twiddle[0], twiddle[1]
         turned = []
         for j in range(STEP):
-            re = mid[:outer, j * LANES : (j + 1) * LANES]
-            im = mid[outer:, j * LANES : (j + 1) * LANES]
+            re = half[:outer, j * LANES : (j + 1) * LANES]
+            im = half[outer:, j * LANES : (j + 1) * LANES]
             turned.append(
                 jnp.concatenate(
                     [(re * tc + im * ts).astype(BF16), (im * tc - re * ts).astype(BF16)], axis=1
@@ -340,13 +397,29 @@
                 zero = jnp.zeros((1, LANES), F32)
                 rounded = full.astype(BF16)
                 exact = rounded.astype(F32)
+                pieces = []
                 for h in range(pols):
                     low, high = h * half_rows, (h + 1) * half_rows
-                    image[ch, h, part, r] = rounded[low:high]
                     before = exact[low - 1 : low] if h > 0 else zero
                     after = exact[high : high + 1] if h < pols - 1 else zero
-                    edge[ch, h, part, r, 0:1] = before
-                    edge[ch, h, part, r, 1:2] = after
+                    pieces.append((exact[low:high], before, after))
+                for k in range(pols):
+                    main, before, after = pieces[k]
+                    for p in range(1, pols):
+                        mine = pol_i == p
+                        other = pieces[(p + k) % pols]
+                        main = jnp.where(mine, other[0], main)
+                        before = jnp.where(mine, other[1], before)
+                        after = jnp.where(mine, other[2], after)
+                    if k == 0:
+                        chan = pol_i * chans + ch
+                        quad[chan, part, HALF + r] = main.astype(BF16)
+                        quad_edge[chan, part, HALF + r, 0:1] = before
+                        quad_edge[chan, part, HALF + r, 1:2] = after
+                    else:
+                        image[ch, k - 1, part, r] = main.astype(BF16)
+                        edge[ch, k - 1, part, r, 0:1] = before
+                        edge[ch, k - 1, part, r, 1:2] = after
 
     def loop(count, start, fun):
         def body(i, carry):
@@ -354,60 +427,12 @@
             return carry
 
         lax.fori_loop(0, count, body, 0)
-
-    sides = ((0, me > 0), (1, me < groups - 1))
 
     def relays(array, sems, recvs, ch, side):
         @pl.when(sides[side][1])
         def _():
             for o in range(pols):
                 relay(array, sems, recvs, o * chans + ch, side).start()
-
-    quads = bins // STEP
-
-    def finish_exchange(ch):
-        for quad_i in range(quads):
-            for o in range(pols):
-                x_copy(ch, quad_i, o, o).wait_recv()
-            if quad_i == 0:
-                relays(quad, r_send, r_recv, ch, 0)
-        relays(quad, r_send, r_recv, ch, 1)
-        for o in range(pols):
-            e_copy(ch, o, o).wait_recv()
-        for side in range(2):
-            relays(quad_edge, f_send, f_recv, ch, side)
-
-    for ch in range(chans):
-        unpack(ch)
-        for part in range(SMAX // STEP):
-            forward(ch, part)
-
-            @pl.when(me > 0)
-            def _(ch=ch, part=part):
-                halo_copy(ch, part).start()
-
-        for g in range(SMAX // STEP, quads):
-            forward(ch, g)
-        if ch > 0:
-            finish_exchange(ch - 1)
-        for quad_i in range(quads):
-            late = quad_i - (quads - SMAX // STEP)
-            if late >= 0:
-
-                @pl.when(me < groups - 1)
-                def _(ch=ch, late=late):
-                    halo_copy(ch, late).wait_recv()
-
-            inverse(ch, quad_i * STEP // RBLK, quad_i)
-            if quad_i == quads - 1:
-                for k in range(1, pols):
-                    e_copy(ch, lax.rem(pol_i + k, pols), pol_i).start()
-                e_own(ch).start()
-            for k in range(1, pols):
-                x_copy(ch, quad_i, lax.rem(pol_i + k, pols), pol_i).start()
-            x_own(ch, quad_i).start()
-
-    finish_exchange(chans - 1)
 
     def pauli(source, target, r):
         v = [[source[c, part, r].astype(F32) for part in range(2)] for c in range(4)]
@@ -425,14 +450,98 @@
         pauli(quad, cells, r)
         pauli(quad_edge, cells_edge, r)
 
-    loop(bins, HALF, cell_row)
-    for side, cond in ((0, me < groups - 1), (1, me > 0)):
-
-        @pl.when(cond)
-        def _(side=side):
-            for chan in range(4):
-                relay(quad, r_send, r_recv, chan, side).wait_recv()
-                relay(quad_edge, f_send, f_recv, chan, side).wait_recv()
+    def pass_on(ch, side):
+        landed(ch, rims[side])
+        relays(quad, r_send, r_recv, ch, side)
+        relays(quad_edge, f_send, f_recv, ch, side)
+
+    def produce(ch, blk):
+        inverse(ch, blk * STEP // RBLK, blk)
+        for k in range(1, pols):
+            e_copy(ch, blk, k).start()
+            x_copy(ch, blk, k).start()
+
+    def take_halo(ch, part):
+        @pl.when((me < groups - 1) & (me != mid - 1))
+        def _():
+            halo_copy(ch, part).wait_recv()
+
+        @pl.when(me == mid - 1)
+        def _():
+            slot = units + ch * halos + part
+            z_landed(slot)
+            unpack(slot)
+            forward(ch, quads + part)
+
+    rims = (0, quads - 1)
+    late = list(range(quads - halos, quads))
+    for ch in range(chans):
+        for part in range(quads):
+            unit = ch * quads + part
+            z_landed(unit)
+            send_step(unit + AHEAD + mylag)
+            unpack(unit)
+            forward(ch, part)
+            if part < halos:
+
+                @pl.when((me > 0) & (me != mid))
+                def _(ch=ch, part=part):
+                    halo_copy(ch, part).start()
+
+            if part >= halos:
+                produce(ch, part - halos)
+            if ch > 0:
+                if part < halos:
+                    take_halo(ch - 1, part)
+                    produce(ch - 1, late[part])
+                if part == halos - 1:
+                    pass_on(ch - 1, 0)
+                if part == quads - 2:
+                    pass_on(ch - 1, 1)
+                    x_sent(ch - 1)
+            if unit >= DRAIN:
+                z_sent(unit - DRAIN)
+
+    last = chans - 1
+    for part in range(halos):
+        take_halo(last, part)
+    for blk in late[::-1]:
+        produce(last, blk)
+    for ch in range(chans):
+        if ch < last:
+            for blk in range(1, quads - 1):
+                landed(ch, blk)
+
+        @pl.when((me > 0) & (me != mid))
+        def _(ch=ch):
+            for part in range(halos):
+                halo_copy(ch, part).wait_send()
+
+    for unit in range(max(0, units - DRAIN), units):
+        z_sent(unit)
+
+    @pl.when(me != mid - 1)
+    def _():
+        for slot in range(units, units + chans * halos):
+            if mid > 0:
+                some = recv.at[slot, 0]
+                pltpu.make_async_copy(some, some, z_send.at[slot]).wait()
+
+    for side in range(2):
+        pass_on(last, side)
+        loop(STEP, HALF + rims[side] * STEP, cell_row)
+    for blk in range(1, quads - 1):
+        landed(last, blk)
+        loop(STEP, HALF + blk * STEP, cell_row)
+    x_sent(last)
+    for array, sems, recvs in ((quad, r_send, r_recv), (quad_edge, f_send, f_recv)):
+        relayed(array, sems)
+        rows = array.at[:, :, pl.ds(0, HALF)]
+        for side, cond in ((0, me < groups - 1), (1, me > 0)):
+
+            @pl.when(cond)
+            def _(side=side, rows=rows, recvs=recvs):
+                pltpu.make_async_copy(rows, rows, recvs.at[side]).wait()
 
     loop(HALF, 0, cell_row)
     loop(HALF, bins + HALF, cell_row)
@@ -470,33 +579,6 @@
     for i in range(9):
         component(i)
 
-    for ch in range(chans):
-
-        def sent(k, carry, ch=ch):
-            z_copy(ch, lax.rem(me + k, groups), me).wait_send()
-            return carry
-
-        lax.fori_loop(1, groups, sent, 0)
-
-        @pl.when(me > 0)
-        def _(ch=ch):
-            for part in range(SMAX // STEP):
-                halo_copy(ch, part).wait_send()
-
-        for k in range(1, pols):
-            dest = lax.rem(pol_i + k, pols)
-            for quad_i in range(quads):
-                x_copy(ch, quad_i, dest, pol_i).wait_send()
-            e_copy(ch, dest, pol_i).wait_send()
-
-    for side, cond in sides:
-
-        @pl.when(cond)
-        def _(side=side):
-            for chan in range(4):
-                relay(quad, r_send, r_recv, chan, side).wait_send()
-                relay(quad_edge, f_send, f_recv, chan, side).wait_send()
-
 
 def shards(echoes, migration, fm_rate):
     rng_size = lax.axis_size("rng")
@@ -507,6 +589,7 @@
     bins = echoes.shape[2] // groups
     outer = groups * pulses // LANES
     half_rows = outer // pols
+    units = chans * (bins // STEP)
     consts = tables(outer)
     vmem = pl.BlockSpec(memory_space=pltpu.VMEM)
     anywhere = pl.BlockSpec(memory_space=pltpu.HBM)
@@ -526,11 +609,11 @@
             pltpu.VMEM(migration.shape, jnp.int32),
             *(pltpu.VMEM(table.shape, table.dtype) for table in consts),
             dma((1 + len(consts),)),
-            pltpu.VMEM((chans, groups, 2, bins, pulses), BF16),
-            pltpu.VMEM((2 * outer * bins, LANES), F32),
+            pltpu.VMEM((units + chans * (SMAX // STEP), groups, 2, STEP, pulses), BF16),
+            pltpu.VMEM((2 * outer * STEP, LANES), F32),
             pltpu.VMEM((chans, 2, bins + SMAX, outer, LANES), BF16),
-            pltpu.VMEM((chans, pols, 2, bins, half_rows, LANES), BF16),
-            pltpu.VMEM((chans, pols, 2, bins, 2, LANES), F32),
+            pltpu.VMEM((chans, pols - 1, 2, bins, half_rows, LANES), BF16),
+            pltpu.VMEM((chans, pols - 1, 2, bins, 2, LANES), F32),
             pltpu.VMEM((4, 2, tall, half_rows, LANES), BF16),
             pltpu.VMEM((4, 2, tall, 2, LANES), F32),
             pltpu.VMEM((migration.shape[0], outer, LANES), BF16),
@@ -541,18 +624,18 @@
             pltpu.VMEM((9, tall, 2, LANES), F32),
             pltpu.VMEM((SLOTS, bins, half_rows + 16, LANES), F32),
             pltpu.VMEM((SLOTS, bins * half_rows, LANES), F32),
-            dma((chans, groups)),
-            dma((chans, groups)),
+            dma((units + chans * (SMAX // STEP),)),
+            dma((units + chans * (SMAX // STEP),)),
             dma((chans, SMAX // STEP)),
             dma((chans, SMAX // STEP)),
-            dma((chans, bins // STEP, pols)),
-            dma((chans, bins // STEP, pols)),
-            dma((chans, pols)),
-            dma((chans, pols)),
-            dma((4, 2)),
-            dma((4, 2)),
-            dma((4, 2)),
-            dma((4, 2)),
+            dma((chans,)),
+            dma((chans, bins // STEP)),
+            dma((chans,)),
+            dma((chans, bins // STEP)),
+            dma((2,)),
+            dma((2,)),
+            dma((2,)),
+            dma((2,)),
         ],
         compiler_params=pltpu.CompilerParams(
             collective_id=0, has_side_effects=True, vmem_limit_bytes=58 * 1024 * 1024

time: 48.9 us -> 44.6 us (0.912)
  the two profiles are of different devices: /device:TPU:13 before, /device:TPU:1 now
where the time goes in v1:
time: 44.6 us; the launch traced here: 44.5 us
  Pallas kernels  43.4 us (97%)
  local copies, waits for them, and re-layouts  1.02 us (2%)
    pallas_call x1, Pallas kernels, shards(): pl.pallas_call(functools.partial(kernel, chans, groups, pols, bins, outer...  43.4 us
    unnamed x1, local copies, waits for them, and re-layouts  1.02 us

profile of v1, /device:TPU:1, one launch (start us, length us, event | category | flops | bytes accessed | tf_op | source)
XLA Modules:
  0.0 44.5 jit_solution(13685468272882925980)
XLA Ops:
  0.0 43.4 %shard_map.64 = bf16[9,16,4096]{2,1,0:T(8,128)(2,1)S(1)} custom-call(bf16[2,2,128,1024]{3,2,1,0:T(8,128)(2,1)} %echo.1, s32[2,8192]{1,0:T(2,128)} %mig_hbm.1, f32[16]{0:T(128)} %rate.1, bf16[768,256]{1,0:T(8,128)(2,1)} %constant.6.clone.wide_hbm, bf16[384,128]{1,0:T(8,128)(2,1)} %constant.7.clone.slim_hbm, f32[4,64,128]{2,1,0:T(8,128)} %constant.8.clone.twiddle_hbm), custom_call_target="tpu_custom_call" | custom-call | tf_op jit(solution)/shard_map/pallas_call | solution.py:598
  43.5 1.0 %copy.8 = bf16[9,16,4096]{2,1,0:T(8,128)(2,1)} copy(bf16[9,16,4096]{2,1,0:T(8,128)(2,1)S(1)} %shard_map.64) | data formatting | bytes 2359296

commit v2 on v1

--- a/solution.py
+++ b/solution.py
@@ -17,10 +17,10 @@
 STEP = 4
 SLOTS = 3
 AHEAD = 3
-LAG = 1
+LAG = 2
 FIRST = 0
-RAW = 1
-DRAIN = AHEAD + LAG + FIRST
+RAW = 5
+REVERSE = False
 ROOT_HALF = 0.7071067811865476
 MESH = pl.DeviceIdType.MESH
 F32 = jnp.float32
@@ -140,7 +140,7 @@
         return pltpu.make_async_remote_copy(
             src_ref=echo.at[ch, :, pl.ds(start, STEP), :],
             dst_ref=recv.at[slot, me],
-            send_sem=z_send.at[slot],
+            send_sem=z_send.at[slot // units],
             recv_sem=z_recv.at[slot],
             device_id=member(q),
             device_id_type=MESH,
@@ -156,15 +156,14 @@
     def z_landed(slot):
         pltpu.make_async_copy(recv.at[slot], recv.at[slot], z_recv.at[slot]).wait()
 
-    def z_sent(slot):
-        some = recv.at[slot, pl.ds(0, groups - 1)]
-        pltpu.make_async_copy(some, some, z_send.at[slot]).wait()
+    def place(core):
+        return rng_size - 1 - core if REVERSE else core
 
     def send_step(step):
         def to_layer(layer, near):
             for j in range(rng_size):
                 q = layer * rng_size + j
-                unit = step - LAG * j - FIRST * jnp.minimum(layer, 1)
+                unit = step - LAG * place(j) - FIRST * jnp.minimum(layer, 1)
                 valid = (unit >= 0) & (unit < units)
                 if near:
 
@@ -191,7 +190,7 @@
 
         lax.fori_loop(0, depth - 1, send_echo, 0)
         to_layer(pulse_i, True)
-        early = step - LAG - FIRST - RAW
+        early = step - FIRST - RAW
         slot = units + early // quads * halos + lax.rem(early, quads)
         valid = (early >= 0) & (early < units) & (lax.rem(early, quads) < halos)
         if mid > 0:
@@ -204,7 +203,7 @@
             def _():
                 z_copy(early, mid, slot, mid - 1).start()
 
-    mylag = LAG * rng_i + FIRST * jnp.minimum(pulse_i, 1)
+    mylag = LAG * place(rng_i) + FIRST * jnp.minimum(pulse_i, 1)
 
     def opening(step, carry):
         send_step(step)
@@ -263,7 +262,7 @@
         return pltpu.make_async_remote_copy(
             src_ref=spec.at[ch, :, pl.ds(part * STEP, STEP)],
             dst_ref=spec.at[ch, :, pl.ds(bins + part * STEP, STEP)],
-            send_sem=h_send.at[ch, part],
+            send_sem=h_send,
             recv_sem=h_recv.at[ch, part],
             device_id=member(jnp.maximum(me - 1, 0)),
             device_id_type=MESH,
@@ -273,7 +272,7 @@
         return pltpu.make_async_remote_copy(
             src_ref=image.at[ch, k - 1, :, pl.ds(blk * STEP, STEP)],
             dst_ref=quad.at[pol_i * chans + ch, :, pl.ds(HALF + blk * STEP, STEP)],
-            send_sem=x_send.at[ch],
+            send_sem=x_send,
             recv_sem=x_recv.at[ch, blk],
             device_id={"pol": lax.rem(pol_i + k, pols)},
             device_id_type=MESH,
@@ -283,7 +282,7 @@
         return pltpu.make_async_remote_copy(
             src_ref=edge.at[ch, k - 1, :, pl.ds(blk * STEP, STEP)],
             dst_ref=quad_edge.at[pol_i * chans + ch, :, pl.ds(HALF + blk * STEP, STEP)],
-            send_sem=e_send.at[ch],
+            send_sem=e_send,
             recv_sem=e_recv.at[ch, blk],
             device_id={"pol": lax.rem(pol_i + k, pols)},
             device_id_type=MESH,
@@ -296,12 +295,6 @@
             few = quad_edge.at[pl.ds(0, pols - 1), :, rows]
             pltpu.make_async_copy(some, some, x_recv.at[ch, blk]).wait()
             pltpu.make_async_copy(few, few, e_recv.at[ch, blk]).wait()
-
-    def x_sent(ch):
-        if pols > 1:
-            some, few = image.at[ch], edge.at[ch]
-            pltpu.make_async_copy(some, some, x_send.at[ch]).wait()
-            pltpu.make_async_copy(few, few, e_send.at[ch]).wait()
 
     def relay(array, sems, recvs, chan, side):
         take = HALF if side == 0 else bins
@@ -428,12 +421,6 @@
 
         lax.fori_loop(0, count, body, 0)
 
-    def relays(array, sems, recvs, ch, side):
-        @pl.when(sides[side][1])
-        def _():
-            for o in range(pols):
-                relay(array, sems, recvs, o * chans + ch, side).start()
-
     def pauli(source, target, r):
         v = [[source[c, part, r].astype(F32) for part in range(2)] for c in range(4)]
         k1 = [(v[0][i] + v[3][i]) * ROOT_HALF for i in range(2)]
@@ -450,16 +437,26 @@
         pauli(quad, cells, r)
         pauli(quad_edge, cells_edge, r)
 
+    def rim_copies(ch, side, owner):
+        @pl.when(sides[side][1])
+        def _():
+            relay(quad, r_send, r_recv, owner * chans + ch, side).start()
+            relay(quad_edge, f_send, f_recv, owner * chans + ch, side).start()
+
     def pass_on(ch, side):
         landed(ch, rims[side])
-        relays(quad, r_send, r_recv, ch, side)
-        relays(quad_edge, f_send, f_recv, ch, side)
+        for k in range(side, pols):
+            rim_copies(ch, side, lax.rem(pol_i + k, pols))
 
     def produce(ch, blk):
         inverse(ch, blk * STEP // RBLK, blk)
         for k in range(1, pols):
             e_copy(ch, blk, k).start()
             x_copy(ch, blk, k).start()
+
+        @pl.when(blk == quads - 1)
+        def _():
+            rim_copies(ch, 1, pol_i)
 
     def take_halo(ch, part):
         @pl.when((me < groups - 1) & (me != mid - 1))
@@ -488,96 +485,139 @@
                 def _(ch=ch, part=part):
                     halo_copy(ch, part).start()
 
-            if part >= halos:
+            if part >= halos and (part < quads - 1 or ch < chans - 1):
                 produce(ch, part - halos)
             if ch > 0:
                 if part < halos:
                     take_halo(ch - 1, part)
                     produce(ch - 1, late[part])
-                if part == halos - 1:
-                    pass_on(ch - 1, 0)
-                if part == quads - 2:
-                    pass_on(ch - 1, 1)
-                    x_sent(ch - 1)
-            if unit >= DRAIN:
-                z_sent(unit - DRAIN)
+
+    def range_sum(x, count):
+        two = x[:-1] + x[1:]
+        four = two[:-2] + two[2:]
+        return four[:count] + two[4 : 4 + count] + x[6 : 6 + count]
+
+    def component(i, low, high):
+        slot, count = i % SLOTS, high - low
+        tall = slice(low, high + 2 * HALF)
+        for j in range(half_rows // 8):
+            padded[slot, :count, 8 + j * 8 : 16 + j * 8, :] = range_sum(
+                cells[i, tall, j * 8 : (j + 1) * 8, :], count
+            )
+        rim = range_sum(cells_edge[i, tall], count)
+        padded[slot, :count, 7:8, :] = rim[:, 0:1, :]
+        padded[slot, :count, 8 + half_rows : 9 + half_rows, :] = rim[:, 1:2, :]
+        center = padded[slot, :count, 8 : 8 + half_rows, :]
+        lane = lax.broadcasted_iota(jnp.int32, (count, half_rows, LANES), 2)
+        side = jnp.where(
+            lane < LANES // 2,
+            padded[slot, :count, 9 : 9 + half_rows, :],
+            padded[slot, :count, 7 : 7 + half_rows, :],
+        )
+        flat = (count * half_rows, LANES)
+        both = jnp.concatenate(
+            [center.reshape(flat).astype(BF16), side.reshape(flat).astype(BF16)], axis=1
+        )
+        total = jnp.dot(both, band[...], preferred_element_type=F32)
+        total = total * (1.0 / (WIN * WIN))
+        for r in range(count):
+            start = (low + r) * (half_rows + 8)
+            result[i, start : start + half_rows] = total[r * half_rows : (r + 1) * half_rows]
+
+    def window(low, high):
+        for i in range(9):
+            component(i, low, high)
+
+    def take_rim(side):
+        @pl.when((me < groups - 1) if side == 0 else (me > 0))
+        def _():
+            for array, recvs in ((quad, r_recv), (quad_edge, f_recv)):
+                rows = array.at[:, :, pl.ds(0, HALF)]
+                pltpu.make_async_copy(rows, rows, recvs.at[side]).wait()
+
+        loop(HALF, bins + HALF if side == 0 else 0, cell_row)
+
+    def take_quad(blk):
+        landed(last, blk)
+        loop(STEP, HALF + blk * STEP, cell_row)
 
     last = chans - 1
-    for part in range(halos):
-        take_halo(last, part)
-    for blk in late[::-1]:
+    lagging = place(rng_i) == rng_size - 1
+    leading = place(rng_i) != rng_size - 1
+    inner = quads - 1 - halos
+
+    def take_halos():
+        for part in range(halos):
+            take_halo(last, part)
+
+    pl.when(lagging)(take_halos)
+    produce(last, jnp.where(lagging, quads - 1, inner))
+    pl.when(leading)(take_halos)
+    produce(last, jnp.where(lagging, inner, quads - 1))
+    for blk in late[:-1]:
         produce(last, blk)
     for ch in range(chans):
         if ch < last:
+            for side in range(2):
+                pass_on(ch, side)
             for blk in range(1, quads - 1):
                 landed(ch, blk)
-
-        @pl.when((me > 0) & (me != mid))
-        def _(ch=ch):
-            for part in range(halos):
-                halo_copy(ch, part).wait_send()
-
-    for unit in range(max(0, units - DRAIN), units):
-        z_sent(unit)
+    pass_on(last, 0)
+    loop(STEP, HALF, cell_row)
+    early = (quads - halos) * STEP - HALF
+
+    def take_rim_quad():
+        pass_on(last, 1)
+        loop(STEP, HALF + (quads - 1) * STEP, cell_row)
+
+    @pl.when(lagging)
+    def _():
+        take_rim_quad()
+        for blk in range(1, quads - halos):
+            take_quad(blk)
+        take_rim(1)
+        window(0, early)
+        for blk in range(quads - halos, quads - 1):
+            take_quad(blk)
+        take_rim(0)
+        window(early, bins)
+
+    @pl.when(leading)
+    def _():
+        for blk in range(1, quads - halos):
+            take_quad(blk)
+        take_rim_quad()
+        for blk in range(quads - halos, quads - 1):
+            take_quad(blk)
+        window(HALF, bins - HALF)
+        take_rim(0)
+        window(bins - HALF, bins)
+        take_rim(1)
+        window(0, HALF)
+
+    for i in range(9):
+        for a in range(half_rows):
+            piece = result[i, pl.ds(a, bins, stride=half_rows + 8), :]
+            out[i, :, a * LANES : (a + 1) * LANES] = piece.astype(BF16)
+
+    def drain(array, sem):
+        pltpu.make_async_copy(array, array, sem).wait()
+
+    drain(recv.at[pl.ds(0, units), pl.ds(0, groups - 1)], z_send.at[0])
 
     @pl.when(me != mid - 1)
     def _():
-        for slot in range(units, units + chans * halos):
-            if mid > 0:
-                some = recv.at[slot, 0]
-                pltpu.make_async_copy(some, some, z_send.at[slot]).wait()
-
-    for side in range(2):
-        pass_on(last, side)
-        loop(STEP, HALF + rims[side] * STEP, cell_row)
-    for blk in range(1, quads - 1):
-        landed(last, blk)
-        loop(STEP, HALF + blk * STEP, cell_row)
-    x_sent(last)
-    for array, sems, recvs in ((quad, r_send, r_recv), (quad_edge, f_send, f_recv)):
-        relayed(array, sems)
-        rows = array.at[:, :, pl.ds(0, HALF)]
-        for side, cond in ((0, me < groups - 1), (1, me > 0)):
-
-            @pl.when(cond)
-            def _(side=side, rows=rows, recvs=recvs):
-                pltpu.make_async_copy(rows, rows, recvs.at[side]).wait()
-
-    loop(HALF, 0, cell_row)
-    loop(HALF, bins + HALF, cell_row)
-
-    def range_sum(x):
-        two = x[:-1] + x[1:]
-        four = two[:-2] + two[2:]
-        return four[:bins] + two[4 : 4 + bins] + x[6 : 6 + bins]
-
-    lane = lax.broadcasted_iota(jnp.int32, (bins, half_rows, LANES), 2)
-
-    def component(i):
-        slot = i % SLOTS
-        for j in range(half_rows // 8):
-            padded[slot, :, 8 + j * 8 : 16 + j * 8, :] = range_sum(cells[i, :, j * 8 : (j + 1) * 8, :])
-        rim = range_sum(cells_edge[i])
-        padded[slot, :, 7:8, :] = rim[:, 0:1, :]
-        padded[slot, :, 8 + half_rows : 9 + half_rows, :] = rim[:, 1:2, :]
-        mid = padded[slot, :, 8 : 8 + half_rows, :]
-        side = jnp.where(
-            lane < LANES // 2,
-            padded[slot, :, 9 : 9 + half_rows, :],
-            padded[slot, :, 7 : 7 + half_rows, :],
-        )
-        flat = (bins * half_rows, LANES)
-        both = jnp.concatenate(
-            [mid.reshape(flat).astype(BF16), side.reshape(flat).astype(BF16)], axis=1
-        )
-        total = jnp.dot(both, band[...], preferred_element_type=F32)
-        result[slot] = total * (1.0 / (WIN * WIN))
-        for a in range(half_rows):
-            piece = result[slot, pl.ds(a, bins, stride=half_rows), :]
-            out[i, :, a * LANES : (a + 1) * LANES] = piece.astype(BF16)
-
-    for i in range(9):
-        component(i)
+        drain(recv.at[pl.ds(0, chans * halos), 0], z_send.at[1])
+
+    @pl.when((me > 0) & (me != mid))
+    def _():
+        drain(spec.at[:, :, pl.ds(0, SMAX)], h_send)
+
+    if pols > 1:
+        drain(image, x_send)
+        drain(edge, e_send)
+    relayed(quad, r_send)
+    relayed(quad_edge, f_send)
 
 
 def shards(echoes, migration, fm_rate):
@@ -623,14 +663,14 @@
             pltpu.VMEM((9, tall, half_rows, LANES), F32),
             pltpu.VMEM((9, tall, 2, LANES), F32),
             pltpu.VMEM((SLOTS, bins, half_rows + 16, LANES), F32),
-            pltpu.VMEM((SLOTS, bins * half_rows, LANES), F32),
+            pltpu.VMEM((9, bins * (half_rows + 8), LANES), F32),
+            dma((2,)),
             dma((units + chans * (SMAX // STEP),)),
-            dma((units + chans * (SMAX // STEP),)),
+            dma,
             dma((chans, SMAX // STEP)),
-            dma((chans, SMAX // STEP)),
-            dma((chans,)),
+            dma,
             dma((chans, bins // STEP)),
-            dma((chans,)),
+            dma,
             dma((chans, bins // STEP)),
             dma((2,)),
             dma((2,)),

time: 44.6 us -> 39.9 us (0.89)
  Pallas kernels: 43.4 us -> 38.7 us
    pallas_call x1, Pallas kernels: 43.4 us -> 38.7 us  [shards(): pl.pallas_call(functools.partial(kernel, chans, groups, pols, bins, outer...]
where the time goes in v2:
time: 39.9 us; the launch traced here: 39.8 us
  Pallas kernels  38.7 us (97%)
  local copies, waits for them, and re-layouts  1.02 us (3%)
    pallas_call x1, Pallas kernels, shards(): pl.pallas_call(functools.partial(kernel, chans, groups, pols, bins, outer...  38.7 us
    unnamed x1, local copies, waits for them, and re-layouts  1.02 us

profile of v2, /device:TPU:1, one launch (start us, length us, event | category | flops | bytes accessed | tf_op | source)
XLA Modules:
  0.0 39.8 jit_solution(15920119426166857114)
XLA Ops:
  0.0 38.7 %shard_map.64 = bf16[9,16,4096]{2,1,0:T(8,128)(2,1)S(1)} custom-call(bf16[2,2,128,1024]{3,2,1,0:T(8,128)(2,1)} %echo.1, s32[2,8192]{1,0:T(2,128)} %mig_hbm.1, f32[16]{0:T(128)} %rate.1, bf16[768,256]{1,0:T(8,128)(2,1)} %constant.6.clone.wide_hbm, bf16[384,128]{1,0:T(8,128)(2,1)} %constant.7.clone.slim_hbm, f32[4,64,128]{2,1,0:T(8,128)} %constant.8.clone.twiddle_hbm), custom_call_target="tpu_custom_call" | custom-call | tf_op jit(solution)/shard_map/pallas_call | solution.py:638
  38.7 1.0 %copy.8 = bf16[9,16,4096]{2,1,0:T(8,128)(2,1)} copy(bf16[9,16,4096]{2,1,0:T(8,128)(2,1)S(1)} %shard_map.64) | data formatting | bytes 2359296

commit v3 on v2

--- a/solution.py
+++ b/solution.py
@@ -90,7 +90,7 @@
     mig, wide_t, slim_t, twiddle, t_sem,
     recv, unpacked, spec, image, edge, quad, quad_edge, shifts, mig_rows, cosine, sine,
     cells, cells_edge, padded, result,
-    z_send, z_recv, h_send, h_recv, x_send, x_recv, e_send, e_recv, r_send, r_recv, f_send, f_recv,
+    z_send, z_recv, h_send, h_recv, x_send, x_recv, r_send, r_recv,
 ):
     half_rows = outer // pols
     local_a = outer // groups
@@ -282,19 +282,20 @@
         return pltpu.make_async_remote_copy(
             src_ref=edge.at[ch, k - 1, :, pl.ds(blk * STEP, STEP)],
             dst_ref=quad_edge.at[pol_i * chans + ch, :, pl.ds(HALF + blk * STEP, STEP)],
-            send_sem=e_send,
-            recv_sem=e_recv.at[ch, blk],
+            send_sem=x_send,
+            recv_sem=x_recv.at[ch, blk],
             device_id={"pol": lax.rem(pol_i + k, pols)},
             device_id_type=MESH,
         )
 
+    def drain(array, sem):
+        pltpu.make_async_copy(array, array, sem).wait()
+
+    share = 2 * STEP + 2 * STEP * 2 * 4 // (half_rows * 2)
+
     def landed(ch, blk):
         if pols > 1:
-            rows = pl.ds(HALF + blk * STEP, STEP)
-            some = quad.at[pl.ds(0, pols - 1), :, rows]
-            few = quad_edge.at[pl.ds(0, pols - 1), :, rows]
-            pltpu.make_async_copy(some, some, x_recv.at[ch, blk]).wait()
-            pltpu.make_async_copy(few, few, e_recv.at[ch, blk]).wait()
+            drain(quad.at[pl.ds(0, pols - 1), 0, pl.ds(0, share)], x_recv.at[ch, blk])
 
     def relay(array, sems, recvs, chan, side):
         take = HALF if side == 0 else bins
@@ -310,14 +311,6 @@
         )
 
     sides = ((0, me > 0), (1, me < groups - 1))
-
-    def relayed(array, sems):
-        rows = array.at[:, :, pl.ds(0, HALF)]
-        for side, cond in sides:
-
-            @pl.when(cond)
-            def _(side=side):
-                pltpu.make_async_copy(rows, rows, sems.at[side]).wait()
 
     def unpack(slot):
         def body(p, carry):
@@ -441,7 +434,7 @@
         @pl.when(sides[side][1])
         def _():
             relay(quad, r_send, r_recv, owner * chans + ch, side).start()
-            relay(quad_edge, f_send, f_recv, owner * chans + ch, side).start()
+            relay(quad_edge, r_send, r_recv, owner * chans + ch, side).start()
 
     def pass_on(ch, side):
         landed(ch, rims[side])
@@ -471,6 +464,9 @@
             forward(ch, quads + part)
 
     rims = (0, quads - 1)
+    lagging = place(rng_i) == rng_size - 1
+    leading = place(rng_i) != rng_size - 1
+    prompt = lagging & (me != mid - 1)
     late = list(range(quads - halos, quads))
     for ch in range(chans):
         for part in range(quads):
@@ -487,10 +483,24 @@
 
             if part >= halos and (part < quads - 1 or ch < chans - 1):
                 produce(ch, part - halos)
+            if part == quads - 1 and ch < chans - 1:
+
+                @pl.when(prompt)
+                def _(ch=ch):
+                    for h in range(halos):
+
+                        @pl.when(me < groups - 1)
+                        def _(h=h):
+                            halo_copy(ch, h).wait_recv()
+
+                        produce(ch, late[h])
             if ch > 0:
                 if part < halos:
-                    take_halo(ch - 1, part)
-                    produce(ch - 1, late[part])
+
+                    @pl.when(jnp.logical_not(prompt))
+                    def _(ch=ch, part=part):
+                        take_halo(ch - 1, part)
+                        produce(ch - 1, late[part])
 
     def range_sum(x, count):
         two = x[:-1] + x[1:]
@@ -531,9 +541,7 @@
     def take_rim(side):
         @pl.when((me < groups - 1) if side == 0 else (me > 0))
         def _():
-            for array, recvs in ((quad, r_recv), (quad_edge, f_recv)):
-                rows = array.at[:, :, pl.ds(0, HALF)]
-                pltpu.make_async_copy(rows, rows, recvs.at[side]).wait()
+            drain(quad.at[pl.ds(0, HALF), 0, pl.ds(0, share)], r_recv.at[side])
 
         loop(HALF, bins + HALF if side == 0 else 0, cell_row)
 
@@ -542,8 +550,6 @@
         loop(STEP, HALF + blk * STEP, cell_row)
 
     last = chans - 1
-    lagging = place(rng_i) == rng_size - 1
-    leading = place(rng_i) != rng_size - 1
     inner = quads - 1 - halos
 
     def take_halos():
@@ -577,9 +583,9 @@
             take_quad(blk)
         take_rim(1)
         window(0, early)
+        take_rim(0)
         for blk in range(quads - halos, quads - 1):
             take_quad(blk)
-        take_rim(0)
         window(early, bins)
 
     @pl.when(leading)
@@ -600,9 +606,6 @@
             piece = result[i, pl.ds(a, bins, stride=half_rows + 8), :]
             out[i, :, a * LANES : (a + 1) * LANES] = piece.astype(BF16)
 
-    def drain(array, sem):
-        pltpu.make_async_copy(array, array, sem).wait()
-
     drain(recv.at[pl.ds(0, units), pl.ds(0, groups - 1)], z_send.at[0])
 
     @pl.when(me != mid - 1)
@@ -614,10 +617,13 @@
         drain(spec.at[:, :, pl.ds(0, SMAX)], h_send)
 
     if pols > 1:
-        drain(image, x_send)
-        drain(edge, e_send)
-    relayed(quad, r_send)
-    relayed(quad_edge, f_send)
+        rows = pl.ds(0, share * bins // (2 * STEP))
+        drain(quad.at[pl.ds(0, chans * (pols - 1)), :, rows], x_send)
+    for side, cond in sides:
+
+        @pl.when(cond)
+        def _(side=side):
+            drain(quad.at[pl.ds(0, HALF), 0, pl.ds(0, share)], r_send.at[side])
 
 
 def shards(echoes, migration, fm_rate):
@@ -670,10 +676,6 @@
             dma((chans, SMAX // STEP)),
             dma,
             dma((chans, bins // STEP)),
-            dma,
-            dma((chans, bins // STEP)),
-            dma((2,)),
-            dma((2,)),
             dma((2,)),
             dma((2,)),
         ],

time: 39.9 us -> 39.6 us (level)
  no operation moved by 1% of the time
where the time goes in v3:
time: 39.6 us; the launch traced here: 39.5 us
  Pallas kernels  38.5 us (97%)
  local copies, waits for them, and re-layouts  1.02 us (3%)
    pallas_call x1, Pallas kernels, shards(): pl.pallas_call(functools.partial(kernel, chans, groups, pols, bins, outer...  38.5 us
    unnamed x1, local copies, waits for them, and re-layouts  1.02 us

profile of v3, /device:TPU:1, one launch (start us, length us, event | category | flops | bytes accessed | tf_op | source)
XLA Modules:
  0.0 39.5 jit_solution(7411519496269350295)
XLA Ops:
  0.0 38.5 %shard_map.64 = bf16[9,16,4096]{2,1,0:T(8,128)(2,1)S(1)} custom-call(bf16[2,2,128,1024]{3,2,1,0:T(8,128)(2,1)} %echo.1, s32[2,8192]{1,0:T(2,128)} %mig_hbm.1, f32[16]{0:T(128)} %rate.1, bf16[768,256]{1,0:T(8,128)(2,1)} %constant.6.clone.wide_hbm, bf16[384,128]{1,0:T(8,128)(2,1)} %constant.7.clone.slim_hbm, f32[4,64,128]{2,1,0:T(8,128)} %constant.8.clone.twiddle_hbm), custom_call_target="tpu_custom_call" | custom-call | tf_op jit(solution)/shard_map/pallas_call | solution.py:644
  38.5 1.0 %copy.8 = bf16[9,16,4096]{2,1,0:T(8,128)(2,1)} copy(bf16[9,16,4096]{2,1,0:T(8,128)(2,1)S(1)} %shard_map.64) | data formatting | bytes 2359296

commit v4 on v3

--- a/solution.py
+++ b/solution.py
@@ -83,6 +83,10 @@
     return jnp.asarray(wide, BF16), jnp.asarray(slim, BF16), jnp.asarray(twiddle, F32)
 
 
+def edge_rows(pols):
+    return 1 if pols == 2 else 2
+
+
 def kernel(
     chans, groups, pols, bins, outer, rng_size,
     echo, mig_hbm, rate, wide_hbm, slim_hbm, twiddle_hbm,
@@ -90,9 +94,10 @@
     mig, wide_t, slim_t, twiddle, t_sem,
     recv, unpacked, spec, image, edge, quad, quad_edge, shifts, mig_rows, cosine, sine,
     cells, cells_edge, padded, result,
-    z_send, z_recv, h_send, h_recv, x_send, x_recv, r_send, r_recv,
+    z_send, z_recv, h_send, h_recv, x_send, x_recv, e_send, r_send, r_recv,
 ):
     half_rows = outer // pols
+    rows_out = edge_rows(pols)
     local_a = outer // groups
     pulse_i, rng_i, pol_i = (lax.axis_index(n) for n in ("pulse", "rng", "pol"))
     me = pulse_i * rng_size + rng_i
@@ -106,8 +111,6 @@
             ((mig_hbm, mig), (slim_hbm, slim_t), (twiddle_hbm, twiddle), (wide_hbm, wide_t))
         )
     ]
-    for fetch in fetches:
-        fetch.start()
     two = 2 * outer
     first_t, last_t = slim_t.at[0:two, 0:two], slim_t.at[two : 2 * two, 0:two]
     fwd_t, inv_t = wide_t.at[0 : 2 * LANES], wide_t.at[2 * LANES : 4 * LANES]
@@ -126,6 +129,8 @@
         pl.semaphore_signal(
             barrier, inc=1, device_id={"pol": lax.rem(pol_i + k, pols)}, device_id_type=MESH
         )
+    for fetch in fetches:
+        fetch.start()
     pl.semaphore_wait(barrier, groups - 1 + pols - 1)
 
     depth = groups // rng_size
@@ -216,12 +221,12 @@
         def _():
             spec[:, :, bins:, :, :] = jnp.zeros((chans, 2, SMAX, outer, LANES), BF16)
             quad[:, :, HALF + bins :, :, :] = jnp.zeros((4, 2, HALF, half_rows, LANES), BF16)
-            quad_edge[:, :, HALF + bins :, :, :] = jnp.zeros((4, 2, HALF, 2, LANES), F32)
+            quad_edge[:, :, HALF + bins :, :, :] = jnp.zeros((4, 2, HALF, rows_out, LANES), F32)
 
         @pl.when(me == 0)
         def _():
             quad[:, :, :HALF, :, :] = jnp.zeros((4, 2, HALF, half_rows, LANES), BF16)
-            quad_edge[:, :, :HALF, :, :] = jnp.zeros((4, 2, HALF, 2, LANES), F32)
+            quad_edge[:, :, :HALF, :, :] = jnp.zeros((4, 2, HALF, rows_out, LANES), F32)
 
     zero_edges()
     for fetch in fetches:
@@ -282,7 +287,7 @@
         return pltpu.make_async_remote_copy(
             src_ref=edge.at[ch, k - 1, :, pl.ds(blk * STEP, STEP)],
             dst_ref=quad_edge.at[pol_i * chans + ch, :, pl.ds(HALF + blk * STEP, STEP)],
-            send_sem=x_send,
+            send_sem=e_send,
             recv_sem=x_recv.at[ch, blk],
             device_id={"pol": lax.rem(pol_i + k, pols)},
             device_id_type=MESH,
@@ -291,11 +296,12 @@
     def drain(array, sem):
         pltpu.make_async_copy(array, array, sem).wait()
 
-    share = 2 * STEP + 2 * STEP * 2 * 4 // (half_rows * 2)
+    share = 2 * STEP * half_rows // 16 + 2 * STEP * rows_out * 4 // (16 * 2)
+    part_row = pl.ds(0, 16)
 
     def landed(ch, blk):
         if pols > 1:
-            drain(quad.at[pl.ds(0, pols - 1), 0, pl.ds(0, share)], x_recv.at[ch, blk])
+            drain(quad.at[pl.ds(0, pols - 1), 0, pl.ds(0, share), part_row], x_recv.at[ch, blk])
 
     def relay(array, sems, recvs, chan, side):
         take = HALF if side == 0 else bins
@@ -388,24 +394,26 @@
                     low, high = h * half_rows, (h + 1) * half_rows
                     before = exact[low - 1 : low] if h > 0 else zero
                     after = exact[high : high + 1] if h < pols - 1 else zero
-                    pieces.append((exact[low:high], before, after))
+                    outside = [before, after]
+                    if rows_out == 1:
+                        outside = [after if h == 0 else before]
+                    pieces.append([exact[low:high]] + outside)
                 for k in range(pols):
-                    main, before, after = pieces[k]
+                    main, *outside = pieces[k]
                     for p in range(1, pols):
                         mine = pol_i == p
                         other = pieces[(p + k) % pols]
                         main = jnp.where(mine, other[0], main)
-                        before = jnp.where(mine, other[1], before)
-                        after = jnp.where(mine, other[2], after)
+                        outside = [jnp.where(mine, o, v) for o, v in zip(other[1:], outside)]
                     if k == 0:
                         chan = pol_i * chans + ch
                         quad[chan, part, HALF + r] = main.astype(BF16)
-                        quad_edge[chan, part, HALF + r, 0:1] = before
-                        quad_edge[chan, part, HALF + r, 1:2] = after
+                        for n, row in enumerate(outside):
+                            quad_edge[chan, part, HALF + r, n : n + 1] = row
                     else:
                         image[ch, k - 1, part, r] = main.astype(BF16)
-                        edge[ch, k - 1, part, r, 0:1] = before
-                        edge[ch, k - 1, part, r, 1:2] = after
+                        for n, row in enumerate(outside):
+                            edge[ch, k - 1, part, r, n : n + 1] = row
 
     def loop(count, start, fun):
         def body(i, carry):
@@ -446,9 +454,7 @@
         for k in range(1, pols):
             e_copy(ch, blk, k).start()
             x_copy(ch, blk, k).start()
-
-        @pl.when(blk == quads - 1)
-        def _():
+        if blk == quads - 1:
             rim_copies(ch, 1, pol_i)
 
     def take_halo(ch, part):
@@ -515,8 +521,12 @@
                 cells[i, tall, j * 8 : (j + 1) * 8, :], count
             )
         rim = range_sum(cells_edge[i, tall], count)
-        padded[slot, :count, 7:8, :] = rim[:, 0:1, :]
-        padded[slot, :count, 8 + half_rows : 9 + half_rows, :] = rim[:, 1:2, :]
+        before, after = rim[:, 0:1, :], rim[:, rows_out - 1 :, :]
+        if rows_out == 1:
+            before = jnp.where(pol_i == 0, 0.0, before)
+            after = jnp.where(pol_i == 0, after, 0.0)
+        padded[slot, :count, 7:8, :] = before
+        padded[slot, :count, 8 + half_rows : 9 + half_rows, :] = after
         center = padded[slot, :count, 8 : 8 + half_rows, :]
         lane = lax.broadcasted_iota(jnp.int32, (count, half_rows, LANES), 2)
         side = jnp.where(
@@ -534,14 +544,23 @@
             start = (low + r) * (half_rows + 8)
             result[i, start : start + half_rows] = total[r * half_rows : (r + 1) * half_rows]
 
-    def window(low, high):
+    def gather(i):
+        for a in range(half_rows):
+            piece = result[i, pl.ds(a, bins, stride=half_rows + 8), :]
+            out[i, :, a * LANES : (a + 1) * LANES] = piece.astype(BF16)
+
+    def window(low, high, finish=False):
         for i in range(9):
             component(i, low, high)
+            if finish and i > 0:
+                gather(i - 1)
+        if finish:
+            gather(8)
 
     def take_rim(side):
         @pl.when((me < groups - 1) if side == 0 else (me > 0))
         def _():
-            drain(quad.at[pl.ds(0, HALF), 0, pl.ds(0, share)], r_recv.at[side])
+            drain(quad.at[pl.ds(0, HALF), 0, pl.ds(0, share), part_row], r_recv.at[side])
 
         loop(HALF, bins + HALF if side == 0 else 0, cell_row)
 
@@ -556,10 +575,9 @@
         for part in range(halos):
             take_halo(last, part)
 
-    pl.when(lagging)(take_halos)
-    produce(last, jnp.where(lagging, quads - 1, inner))
-    pl.when(leading)(take_halos)
-    produce(last, jnp.where(lagging, inner, quads - 1))
+    produce(last, inner)
+    take_halos()
+    produce(last, quads - 1)
     for blk in late[:-1]:
         produce(last, blk)
     for ch in range(chans):
@@ -578,15 +596,15 @@
 
     @pl.when(lagging)
     def _():
-        take_rim_quad()
         for blk in range(1, quads - halos):
             take_quad(blk)
         take_rim(1)
         window(0, early)
+        take_rim_quad()
         take_rim(0)
         for blk in range(quads - halos, quads - 1):
             take_quad(blk)
-        window(early, bins)
+        window(early, bins, True)
 
     @pl.when(leading)
     def _():
@@ -599,12 +617,7 @@
         take_rim(0)
         window(bins - HALF, bins)
         take_rim(1)
-        window(0, HALF)
-
-    for i in range(9):
-        for a in range(half_rows):
-            piece = result[i, pl.ds(a, bins, stride=half_rows + 8), :]
-            out[i, :, a * LANES : (a + 1) * LANES] = piece.astype(BF16)
+        window(0, HALF, True)
 
     drain(recv.at[pl.ds(0, units), pl.ds(0, groups - 1)], z_send.at[0])
 
@@ -617,13 +630,13 @@
         drain(spec.at[:, :, pl.ds(0, SMAX)], h_send)
 
     if pols > 1:
-        rows = pl.ds(0, share * bins // (2 * STEP))
-        drain(quad.at[pl.ds(0, chans * (pols - 1)), :, rows], x_send)
+        drain(image, x_send)
+        drain(edge, e_send)
     for side, cond in sides:
 
         @pl.when(cond)
         def _(side=side):
-            drain(quad.at[pl.ds(0, HALF), 0, pl.ds(0, share)], r_send.at[side])
+            drain(quad.at[pl.ds(0, HALF), 0, pl.ds(0, share), part_row], r_send.at[side])
 
 
 def shards(echoes, migration, fm_rate):
@@ -659,15 +672,15 @@
             pltpu.VMEM((2 * outer * STEP, LANES), F32),
             pltpu.VMEM((chans, 2, bins + SMAX, outer, LANES), BF16),
             pltpu.VMEM((chans, pols - 1, 2, bins, half_rows, LANES), BF16),
-            pltpu.VMEM((chans, pols - 1, 2, bins, 2, LANES), F32),
+            pltpu.VMEM((chans, pols - 1, 2, bins, edge_rows(pols), LANES), F32),
             pltpu.VMEM((4, 2, tall, half_rows, LANES), BF16),
-            pltpu.VMEM((4, 2, tall, 2, LANES), F32),
+            pltpu.VMEM((4, 2, tall, edge_rows(pols), LANES), F32),
             pltpu.VMEM((migration.shape[0], outer, LANES), BF16),
             pltpu.VMEM((outer, LANES), F32),
             pltpu.VMEM((bins, outer, LANES), F32),
             pltpu.VMEM((bins, outer, LANES), F32),
             pltpu.VMEM((9, tall, half_rows, LANES), F32),
-            pltpu.VMEM((9, tall, 2, LANES), F32),
+            pltpu.VMEM((9, tall, edge_rows(pols), LANES), F32),
             pltpu.VMEM((SLOTS, bins, half_rows + 16, LANES), F32),
             pltpu.VMEM((9, bins * (half_rows + 8), LANES), F32),
             dma((2,)),
@@ -676,6 +689,7 @@
             dma((chans, SMAX // STEP)),
             dma,
             dma((chans, bins // STEP)),
+            dma,
             dma((2,)),
             dma((2,)),
         ],

time: 39.6 us -> 39.4 us (level)
  no operation moved by 1% of the time
where the time goes in v4:
time: 39.4 us; the launch traced here: 39.2 us
  Pallas kernels  38.2 us (97%)
  local copies, waits for them, and re-layouts  1.02 us (3%)
    pallas_call x1, Pallas kernels, shards(): pl.pallas_call(functools.partial(kernel, chans, groups, pols, bins, outer...  38.2 us
    unnamed x1, local copies, waits for them, and re-layouts  1.02 us

profile of v4, /device:TPU:1, one launch (start us, length us, event | category | flops | bytes accessed | tf_op | source)
XLA Modules:
  0.0 39.2 jit_solution(9210680156561445904)
XLA Ops:
  0.0 38.2 %shard_map.64 = bf16[9,16,4096]{2,1,0:T(8,128)(2,1)S(1)} custom-call(bf16[2,2,128,1024]{3,2,1,0:T(8,128)(2,1)} %echo.1, s32[2,8192]{1,0:T(2,128)} %mig_hbm.1, f32[16]{0:T(128)} %rate.1, bf16[768,256]{1,0:T(8,128)(2,1)} %constant.6.clone.wide_hbm, bf16[384,128]{1,0:T(8,128)(2,1)} %constant.7.clone.slim_hbm, f32[4,64,128]{2,1,0:T(8,128)} %constant.8.clone.twiddle_hbm), custom_call_target="tpu_custom_call" | custom-call | tf_op jit(solution)/shard_map/pallas_call | solution.py:657
  38.2 1.0 %copy.8 = bf16[9,16,4096]{2,1,0:T(8,128)(2,1)} copy(bf16[9,16,4096]{2,1,0:T(8,128)(2,1)S(1)} %shard_map.64) | data formatting | bytes 2359296
